TPU v7x, 32 devices: a whole 2x2x4 slice. The times are simulated.
32 devices in a mesh: group: 4 (over y, x), fsdp: 2 (over core), tensor: 4 (over z).
Axes of the slice: x: 2, y: 2, z: 4, core: 2. Of those that a mesh axis runs over, the one named last changes fastest.
Arguments:
- patches: bfloat16 [4, 2, 8, 577, 1024], P('group', None, ('fsdp', 'tensor')), may hold values from -6 to 6
- output_grad: bfloat16 [4, 2, 8, 577, 1024], P('group', None, ('fsdp', 'tensor')), may hold values from -6 to 6
- live_counts: int32 [4, 2, 2], P('group'), may hold values from 1 to 4, as said below
- attn_master: float32 [4, 1024, 1024], P(None, 'fsdp', 'tensor')
- mlp_master: float32 [2, 1024, 4096], P(None, 'fsdp', 'tensor')
- vector_master: float32 [12, 1024], replicated
- attn_moments: float32 [4, 2, 4, 1024, 1024], P('group', None, None, 'fsdp', 'tensor'), as said below
- mlp_moments: float32 [4, 2, 2, 1024, 4096], P('group', None, None, 'fsdp', 'tensor'), as said below
- vector_moments: float32 [4, 2, 12, 1024], P('group'), as said below
- attn_outer: float32 [4, 1024, 1024], P(None, 'fsdp', 'tensor'), may hold values from -0.125 to 0.125
- mlp_outer: float32 [2, 1024, 4096], P(None, 'fsdp', 'tensor'), may hold values from -0.125 to 0.125
- vector_outer: float32 [12, 1024], replicated, may hold values from -0.625 to 0.625
Outputs:
- block_output: bfloat16 [4, 2, 8, 577, 1024], P('group', None, ('fsdp', 'tensor'))
- patches_grad: float32 [4, 2, 8, 577, 1024], P('group', None, ('fsdp', 'tensor'))
- attn_inner: float32 [4, 2, 4, 1024, 1024], P('group', None, None, 'fsdp', 'tensor')
- attn_state: float32 [3, 4, 1024, 1024], P(None, None, 'fsdp', 'tensor')
- attn_copy: bfloat16 [4, 1024, 1024], P(None, 'fsdp', 'tensor')
- mlp_inner: float32 [4, 2, 2, 1024, 4096], P('group', None, None, 'fsdp', 'tensor')
- mlp_state: float32 [3, 2, 1024, 4096], P(None, None, 'fsdp', 'tensor')
- mlp_copy: bfloat16 [2, 1024, 4096], P(None, 'fsdp', 'tensor')
- vector_inner: float32 [4, 2, 12, 1024], P('group')
- vector_state: float32 [3, 12, 1024], replicated
- vector_copy: bfloat16 [12, 1024], replicated
Inputs may be any that keep to these rules, and one draw needn't show every extreme that they name: live_counts[g, m, f] images are live, and they stand first, among the f-th block of 4 image slots of micro-batch m in group g; some entry equals 4. `attn_moments`: second moments are positive. `mlp_moments`: second moments are positive. `vector_moments`: second moments are positive.
All inputs are finite; a program needn't handle non-finite values.
Results may differ from a plain program's by a relative error of at most 0.012.
The roundings to bfloat16 on the way count: a program that leaves them out, or rounds other values in their place, can miss the bound.
Values may be sent and summed in bfloat16 or wider, within the bound.
A program may use at most 320 MiB of HBM per device.

v0:
```python
from functools import partial
import jax
import jax.numpy as jnp
from jax import lax
from jax.sharding import PartitionSpec as P

HD = 64
FF = 4096
STEP = 8
EPSILON = 1e-06
INNER_RATE = 0.02
VECTOR_RATE = 0.2
WEIGHT_DECAY = 0.1
OUTER_RATE = 0.7
OUTER_MOMENTUM = 0.9


def normalize(source, gain_row, shift_row):
    centre = source - jnp.mean(source, axis=-1, keepdims=True)
    spread = jnp.mean(centre * centre, axis=-1, keepdims=True)
    return centre * lax.rsqrt(spread + EPSILON) * gain_row + shift_row


def gelu_exact(source):
    return jax.nn.gelu(source, approximate=False)


def gelu_slope(source):
    return (
        0.5 * (1.0 + lax.erf(source * 0.7071067811865476))
        + source * jnp.exp(-0.5 * source * source) * 0.3989422804014327
    )


def inner_adamw(master, gradient, moments, step_rate, decay_rate):
    first_moment = 0.9 * moments[0] + 0.1 * gradient
    second_moment = 0.95 * moments[1] + 0.05 * gradient * gradient
    step_ratio = (
        first_moment / (1.0 - 0.9**STEP) / (jnp.sqrt(second_moment / (1.0 - 0.95**STEP)) + 1e-08)
    )
    return (master - step_rate * (step_ratio + decay_rate * master), second_moment)


def outer_nesterov(master, outer_old, difference):
    momentum = OUTER_MOMENTUM * outer_old + difference
    updated = master - OUTER_RATE * (difference + OUTER_MOMENTUM * momentum)
    return (jnp.stack([difference, momentum, updated]), updated.astype(jnp.bfloat16))


def attend_forward(score_scale, operands):
    queries_low, keys_low, values_low = operands
    scores = (
        jnp.einsum("qhe,khe->hqk", queries_low, keys_low, preferred_element_type=jnp.float32)
        * score_scale
    )
    highest = jnp.max(scores, axis=-1, keepdims=True)
    exponent = jnp.exp(scores - highest)
    totals = jnp.sum(exponent, axis=-1, keepdims=True)
    probs_low = (exponent / totals).astype(jnp.bfloat16)
    attended = jnp.einsum("hqk,khe->qhe", probs_low, values_low, preferred_element_type=jnp.float32)
    return (attended.astype(jnp.bfloat16), (highest + jnp.log(totals))[..., 0])


def attend_backward(score_scale, operands):
    queries_low, keys_low, values_low, log_totals, grad_attended = operands
    scores = (
        jnp.einsum("qhe,khe->hqk", queries_low, keys_low, preferred_element_type=jnp.float32)
        * score_scale
    )
    probs_full = jnp.exp(scores - log_totals[..., None])
    grad_probs = jnp.einsum(
        "qhe,khe->hqk", grad_attended, values_low, preferred_element_type=jnp.float32
    )
    grad_values = jnp.einsum(
        "hqk,qhe->khe",
        probs_full.astype(jnp.bfloat16),
        grad_attended,
        preferred_element_type=jnp.float32,
    )
    weighted = jnp.sum(probs_full * grad_probs, axis=-1, keepdims=True)
    grad_scores = (probs_full * (grad_probs - weighted)).astype(jnp.bfloat16)
    grad_queries = (
        jnp.einsum("hqk,khe->qhe", grad_scores, keys_low, preferred_element_type=jnp.float32)
        * score_scale
    )
    grad_keys = (
        jnp.einsum("hqk,qhe->khe", grad_scores, queries_low, preferred_element_type=jnp.float32)
        * score_scale
    )
    return (
        grad_queries.astype(jnp.bfloat16),
        grad_keys.astype(jnp.bfloat16),
        grad_values.astype(jnp.bfloat16),
    )


def local(
    patches,
    output_grad,
    live_counts,
    attn_master,
    mlp_master,
    vector_master,
    attn_moments,
    mlp_moments,
    vector_moments,
    attn_outer,
    mlp_outer,
    vector_outer,
):
    narrow = jnp.bfloat16
    single = jnp.float32
    tensor_index = lax.axis_index("tensor")
    fsdp_index = lax.axis_index("fsdp")
    micro_count = patches.shape[1]
    local_images = patches.shape[2]
    seq_len = patches.shape[3]
    width = patches.shape[4]
    head_cols = attn_master.shape[2]
    hidden_cols = mlp_master.shape[2]
    score_scale = HD ** (-0.5)
    attn_all, mlp_all = (
        lax.all_gather(attn_master.astype(narrow), "fsdp", axis=1, tiled=True),
        lax.all_gather(mlp_master.astype(narrow), "fsdp", axis=1, tiled=True),
    )
    bias_query = lax.dynamic_slice_in_dim(vector_master[4], tensor_index * head_cols, head_cols)
    bias_value = lax.dynamic_slice_in_dim(vector_master[5], tensor_index * head_cols, head_cols)
    head_width = attn_all.shape[2]
    heads_here = head_width // HD
    bias_hidden = lax.dynamic_slice_in_dim(
        vector_master[8:].reshape(-1), tensor_index * hidden_cols, hidden_cols
    )
    owner_counts = jnp.sum(
        jnp.where(jnp.arange(live_counts.shape[2]) == fsdp_index, live_counts[0], 0), axis=-1
    )
    slot_index = tensor_index * local_images + jnp.arange(local_images)
    alive_all = (slot_index[None, :] < owner_counts[:, None]).astype(single)
    forward_attend = partial(attend_forward, score_scale)
    backward_attend = partial(attend_backward, score_scale)
    qkv_acc = jnp.zeros((3, width, head_width), single)
    out_acc = jnp.zeros((width, head_width), single)
    fc_in_acc = jnp.zeros((width, hidden_cols), single)
    fc_out_acc = jnp.zeros((width, hidden_cols), single)
    hidden_bias_acc = jnp.zeros((hidden_cols,), single)
    query_bias_acc = jnp.zeros((head_width,), single)
    value_bias_acc = jnp.zeros((head_width,), single)
    vector_acc = jnp.zeros((6, width), single)
    outputs_mixed = []
    outputs_grad = []
    for batch_index in range(micro_count):
        inputs = patches[0, batch_index].astype(single)
        alive = alive_all[batch_index][:, None, None]
        normed_one = normalize(inputs, vector_master[0], vector_master[1]).astype(narrow)
        rows_attn = lax.all_gather(normed_one, "tensor", axis=0, tiled=True)
        image_count = rows_attn.shape[0]
        shape_heads = (image_count, seq_len, heads_here, HD)
        projected = jnp.einsum(
            "isd,jde->jise", rows_attn, attn_all[:3], preferred_element_type=single
        )
        queries_low = (projected[0] + bias_query).astype(narrow).reshape(shape_heads)
        keys_low = projected[1].astype(narrow).reshape(shape_heads)
        values_low = (projected[2] + bias_value).astype(narrow).reshape(shape_heads)
        attended, log_totals = lax.map(forward_attend, (queries_low, keys_low, values_low))
        attended = attended.reshape(image_count, seq_len, head_width)
        branch_one = lax.psum_scatter(
            jnp.einsum("ise,de->isd", attended, attn_all[3], preferred_element_type=single),
            "tensor",
            scatter_dimension=0,
            tiled=True,
        )
        resid_one = inputs + branch_one + vector_master[6]
        normed_two = normalize(resid_one, vector_master[2], vector_master[3]).astype(narrow)
        rows_mlp = lax.all_gather(normed_two, "tensor", axis=0, tiled=True)
        pre_act = (
            jnp.einsum("isd,df->isf", rows_mlp, mlp_all[0], preferred_element_type=single)
            + bias_hidden
        )
        hidden = gelu_exact(pre_act).astype(narrow)
        branch_two = lax.psum_scatter(
            jnp.einsum("isf,df->isd", hidden, mlp_all[1], preferred_element_type=single),
            "tensor",
            scatter_dimension=0,
            tiled=True,
        )
        outputs_mixed.append((alive * (resid_one + branch_two + vector_master[7])).astype(narrow))
        grad_out = alive * output_grad[0, batch_index].astype(single)
        rows_grad_two = lax.all_gather(grad_out.astype(narrow), "tensor", axis=0, tiled=True)
        fc_out_acc = fc_out_acc + jnp.einsum(
            "isd,isf->df", rows_grad_two, hidden, preferred_element_type=single
        )
        grad_hidden = jnp.einsum(
            "isd,df->isf", rows_grad_two, mlp_all[1], preferred_element_type=single
        )
        grad_pre = (grad_hidden * gelu_slope(pre_act)).astype(narrow)
        fc_in_acc = fc_in_acc + jnp.einsum(
            "isd,isf->df", rows_mlp, grad_pre, preferred_element_type=single
        )
        hidden_bias_acc = hidden_bias_acc + jnp.sum(grad_pre.astype(single), axis=(0, 1))
        grad_normed_two = lax.psum_scatter(
            jnp.einsum("isf,df->isd", grad_pre, mlp_all[0], preferred_element_type=single),
            "tensor",
            scatter_dimension=0,
            tiled=True,
        )
        unused_two, norm_pull_two = jax.vjp(
            normalize, resid_one, vector_master[2], vector_master[3]
        )
        back_resid, gain_two, shift_two = norm_pull_two(grad_normed_two)
        grad_resid = grad_out + back_resid
        rows_grad_one = lax.all_gather(grad_resid.astype(narrow), "tensor", axis=0, tiled=True)
        out_acc = out_acc + jnp.einsum(
            "isd,ise->de", rows_grad_one, attended, preferred_element_type=single
        )
        grad_attended = jnp.einsum(
            "isd,de->ise", rows_grad_one, attn_all[3], preferred_element_type=single
        ).astype(narrow)
        grad_queries, grad_keys, grad_values = lax.map(
            backward_attend,
            (queries_low, keys_low, values_low, log_totals, grad_attended.reshape(shape_heads)),
        )
        grad_queries = grad_queries.reshape(image_count, seq_len, head_width)
        grad_keys = grad_keys.reshape(image_count, seq_len, head_width)
        grad_values = grad_values.reshape(image_count, seq_len, head_width)
        grad_stack = jnp.stack([grad_queries, grad_keys, grad_values])
        qkv_acc = qkv_acc + jnp.einsum(
            "isd,jise->jde", rows_attn, grad_stack, preferred_element_type=single
        )
        query_bias_acc = query_bias_acc + jnp.sum(grad_queries.astype(single), axis=(0, 1))
        value_bias_acc = value_bias_acc + jnp.sum(grad_values.astype(single), axis=(0, 1))
        summed = jnp.einsum("ise,de->isd", grad_queries, attn_all[0], preferred_element_type=single)
        summed = summed + jnp.einsum(
            "ise,de->isd", grad_keys, attn_all[1], preferred_element_type=single
        )
        grad_normed_one = lax.psum_scatter(
            summed
            + jnp.einsum("ise,de->isd", grad_values, attn_all[2], preferred_element_type=single),
            "tensor",
            scatter_dimension=0,
            tiled=True,
        )
        unused_one, norm_pull_one = jax.vjp(normalize, inputs, vector_master[0], vector_master[1])
        back_inputs, gain_one, shift_one = norm_pull_one(grad_normed_one)
        outputs_grad.append(grad_resid + back_inputs)
        vector_acc = vector_acc + jnp.stack(
            [
                gain_one,
                shift_one,
                gain_two,
                shift_two,
                jnp.sum(grad_resid, axis=(0, 1)),
                jnp.sum(grad_out, axis=(0, 1)),
            ]
        )
    attn_grad_full = jnp.concatenate([qkv_acc, out_acc[None]], 0)
    query_row = lax.dynamic_update_slice_in_dim(
        jnp.zeros((width,), single), query_bias_acc, tensor_index * head_cols, 0
    )
    value_row = lax.dynamic_update_slice_in_dim(
        jnp.zeros((width,), single), value_bias_acc, tensor_index * head_cols, 0
    )
    mlp_grad_cols = jnp.stack([fc_in_acc, fc_out_acc])
    attn_grad, mlp_grad = (
        lax.psum_scatter(attn_grad_full, "fsdp", scatter_dimension=1, tiled=True),
        lax.psum_scatter(mlp_grad_cols, "fsdp", scatter_dimension=1, tiled=True),
    )
    hidden_rows = lax.dynamic_update_slice_in_dim(
        jnp.zeros((FF,), single), hidden_bias_acc, tensor_index * hidden_cols, 0
    ).reshape(-1, width)
    vector_part = jnp.concatenate(
        [vector_acc[:4], jnp.stack([query_row, value_row]), vector_acc[4:], hidden_rows], 0
    )
    vector_grad = lax.psum(vector_part, ("fsdp", "tensor"))
    new_attn, second_attn = inner_adamw(
        attn_master, attn_grad, attn_moments[0], INNER_RATE, WEIGHT_DECAY
    )
    new_mlp, second_mlp = inner_adamw(
        mlp_master, mlp_grad, mlp_moments[0], INNER_RATE, WEIGHT_DECAY
    )
    new_vector, second_vector = inner_adamw(
        vector_master, vector_grad, vector_moments[0], VECTOR_RATE, 0.0
    )
    diff_attn, diff_mlp, diff_vector = lax.psum(
        (attn_master - new_attn, mlp_master - new_mlp, vector_master - new_vector), "group"
    )
    groups = lax.axis_size("group")
    attn_state, attn_copy = outer_nesterov(attn_master, attn_outer, diff_attn / groups)
    mlp_state, mlp_copy = outer_nesterov(mlp_master, mlp_outer, diff_mlp / groups)
    vector_state, vector_copy = outer_nesterov(vector_master, vector_outer, diff_vector / groups)
    block_output = jnp.stack(outputs_mixed)[None]
    patches_grad = jnp.stack(outputs_grad)[None]
    attn_inner = jnp.stack([attn_grad, second_attn])[None]
    mlp_inner = jnp.stack([mlp_grad, second_mlp])[None]
    vector_inner = jnp.stack([vector_grad, second_vector])[None]
    return (
        block_output,
        patches_grad,
        attn_inner,
        attn_state,
        attn_copy,
        mlp_inner,
        mlp_state,
        mlp_copy,
        vector_inner,
        vector_state,
        vector_copy,
    )


def solution(mesh):
    placed = (
        P("group", None, ("fsdp", "tensor"), None, None),
        P("group", None, ("fsdp", "tensor"), None, None),
        P("group", None, None),
        P(None, "fsdp", "tensor"),
        P(None, "fsdp", "tensor"),
        P(),
        P("group", None, None, "fsdp", "tensor"),
        P("group", None, None, "fsdp", "tensor"),
        P("group", None, None, None),
        P(None, "fsdp", "tensor"),
        P(None, "fsdp", "tensor"),
        P(),
    )
    return jax.shard_map(
        local,
        mesh=mesh,
        in_specs=placed,
        out_specs=(
            P("group", None, ("fsdp", "tensor"), None, None),
            P("group", None, ("fsdp", "tensor"), None, None),
            P("group", None, None, "fsdp", "tensor"),
            P(None, None, "fsdp", "tensor"),
            P(None, "fsdp", "tensor"),
            P("group", None, None, "fsdp", "tensor"),
            P(None, None, "fsdp", "tensor"),
            P(None, "fsdp", "tensor"),
            P("group", None, None, None),
            P(),
            P(),
        ),
        check_vma=False,
    )
```

profile of v0, /device:TPU:0, one launch (start us, length us, event | category | flops | bytes accessed | tf_op | source)
XLA Modules:
  0.0 2521.2 jit_solution(1555532051777853854)
XLA Ops:
  23.5 93.8 %all-gather.19.cloned.1.call-done = bf16[4,577,1024]{2,1,0:T(8,128)(2,1)} async-done(((bf16[1,577,1024]{2,1,0:T(8,128)(2,1)}), bf16[4,577,1024]{2,1,0:T(8,128)(2,1)}) %all-gather.19.cloned.1.call-update) | async-done | bytes 4726800 | tf_op jit(solution)/shard_map/all_gather | solution.py:154
  126.6 81.9 %all-gather.11.cloned.1.call-done = bf16[4,577,1024]{2,1,0:T(8,128)(2,1)} async-done(((bf16[1,577,1024]{2,1,0:T(8,128)(2,1)}), bf16[4,577,1024]{2,1,0:T(8,128)(2,1)}) %all-gather.11.cloned.1.call-update) | async-done | bytes 4726800 | tf_op jit(solution)/shard_map/all_gather | solution.py:154
  240.4 25.3 %while.53 = (s32[]{:T(128)}, bf16[4,577,4,64]{1,3,2,0:T(8,128)(2,1)}, f32[4,4,577]{2,1,0:T(4,128)S(1)}, bf16[4,577,4,64]{1,3,2,0:T(8,128)(2,1)}, bf16[4,577,4,64...) while((s32[]{:T(128)}, bf16[4,577,4,64]{1,3,2,0:T(8,128)(2,1)}, ...), condition=%wide.region_16.17_spmd, body=%wide.region_13.16_spmd.sunk | while | flops 353050112 | bytes 17370320 | solution.py:163
  279.1 21.4 while.52
  312.4 122.7 %reduce-scatter.15.cloned.1.call-done = f32[1,577,1024]{2,1,0:T(8,128)} async-done(((f32[4,577,1024]{2,1,0:T(8,128)}), f32[1,577,1024]{2,1,0:T(8,128)}) %reduce-scatter.15.cloned.1.call-update) | async-done | bytes 2363408 | tf_op jit(solution)/shard_map/reduce_scatter | solution.py:165
  435.1 167.2 %reduce-scatter.11.cloned.1.call-done = f32[1,577,1024]{2,1,0:T(8,128)} async-done(((f32[4,577,1024]{2,1,0:T(8,128)}), f32[1,577,1024]{2,1,0:T(8,128)}) %reduce-scatter.11.cloned.1.call-update) | async-done | bytes 2363408 | tf_op jit(solution)/shard_map/reduce_scatter | solution.py:165
  629.3 83.4 %all-gather.21.cloned.1.call-done = bf16[4,577,1024]{2,1,0:T(8,128)(2,1)} async-done(((bf16[1,577,1024]{2,1,0:T(8,128)(2,1)}), bf16[4,577,1024]{2,1,0:T(8,128)(2,1)}) %all-gather.21.cloned.1.call-update) | async-done | bytes 4726800 | tf_op jit(solution)/shard_map/all_gather | solution.py:173
  712.7 10.2 fusion.225
  722.9 80.9 %all-gather.15.cloned.1.call-done = bf16[4,577,1024]{2,1,0:T(8,128)(2,1)} async-done(((bf16[1,577,1024]{2,1,0:T(8,128)(2,1)}), bf16[4,577,1024]{2,1,0:T(8,128)(2,1)}) %all-gather.15.cloned.1.call-update) | async-done | bytes 4726800 | tf_op jit(solution)/shard_map/all_gather | solution.py:173
  803.8 20.2 fusion.210
  824.0 70.3 %all-gather.23.cloned.1.call-done = bf16[4,577,1024]{2,1,0:T(8,128)(2,1)} async-done(((bf16[1,577,1024]{2,1,0:T(8,128)(2,1)}), bf16[4,577,1024]{2,1,0:T(8,128)(2,1)}) %all-gather.23.cloned.1.call-update) | async-done | bytes 4726800 | tf_op jit(solution)/shard_map/all_gather | solution.py:187
  894.3 12.3 convert_reduce_fusion.1
  917.0 67.8 %all-gather.27.cloned.1.call-done = bf16[4,577,1024]{2,1,0:T(8,128)(2,1)} async-done(((bf16[1,577,1024]{2,1,0:T(8,128)(2,1)}), bf16[4,577,1024]{2,1,0:T(8,128)(2,1)}) %all-gather.27.cloned.1.call-update) | async-done | bytes 4726800 | tf_op jit(solution)/shard_map/all_gather | solution.py:187
  984.7 12.5 convert_reduce_fusion
  1007.1 46.6 %fusion.116 = (bf16[4,577,1024]{2,1,0:T(8,128)(2,1)S(1)}, bf16[4,577,1024]{2,1,0:T(8,128)(2,1)}) fusion(f32[4,577,1024]{2,1,0:T(8,128)} %get-tuple-element.421, f32[1024]{0:T(1024)S(1)} %dynamic_slice.61, u8[577,1024]{1,0:T(8,128)(4,1)} %get-tuple-element.249, u8[577,1024]{1,0:T(8,128)(4,1)S(1)} %get-tuple-element.248, ...), kind=kLoop, calls=%fused_computation.127 | loop fusion | flops 333238272 | bytes 30728192 | tf_op jit(solution)/shard_map/convert_element_type | solution.py:178
  1063.8 10.6 fusion.227
  1074.5 74.4 %reduce-scatter.19.cloned.1.call-done = f32[1,577,1024]{2,1,0:T(8,128)} async-done(((f32[4,577,1024]{2,1,0:T(8,128)}), f32[1,577,1024]{2,1,0:T(8,128)}) %reduce-scatter.19.cloned.1.call-update) | async-done | bytes 2363408 | tf_op jit(solution)/shard_map/reduce_scatter | solution.py:199
  1148.9 166.6 %reduce-scatter.23.cloned.1.call-done = f32[1,577,1024]{2,1,0:T(8,128)} async-done(((f32[4,577,1024]{2,1,0:T(8,128)}), f32[1,577,1024]{2,1,0:T(8,128)}) %reduce-scatter.23.cloned.1.call-update) | async-done | bytes 2363408 | tf_op jit(solution)/shard_map/reduce_scatter | solution.py:199
  1320.8 161.4 %reduce-scatter.13.cloned.1.call-done = f32[1,577,1024]{2,1,0:T(8,128)} async-done(((f32[4,577,1024]{2,1,0:T(8,128)}), f32[1,577,1024]{2,1,0:T(8,128)}) %reduce-scatter.13.cloned.1.call-update) | async-done | bytes 2363408 | tf_op jit(solution)/shard_map/reduce_scatter | solution.py:179
  1482.1 167.2 %reduce-scatter.17.cloned.1.call-done = f32[1,577,1024]{2,1,0:T(8,128)} async-done(((f32[4,577,1024]{2,1,0:T(8,128)}), f32[1,577,1024]{2,1,0:T(8,128)}) %reduce-scatter.17.cloned.1.call-update) | async-done | bytes 2363408 | tf_op jit(solution)/shard_map/reduce_scatter | solution.py:179
  1700.8 51.3 %all-gather.29.cloned.1.call-done = bf16[4,577,1024]{2,1,0:T(8,128)(2,1)} async-done(((bf16[1,577,1024]{2,1,0:T(8,128)(2,1)}), bf16[4,577,1024]{2,1,0:T(8,128)(2,1)}) %all-gather.29.cloned.1.call-update) | async-done | bytes 4726800 | tf_op jit(solution)/shard_map/all_gather | solution.py:210
  1760.1 48.8 %while.55 = (s32[]{:T(128)}, bf16[4,577,4,64]{1,3,2,0:T(8,128)(2,1)S(1)}, bf16[4,577,4,64]{1,3,2,0:T(8,128)(2,1)}, bf16[4,577,4,64]{1,3,2,0:T(8,128)(2,1)}, bf16...) while((s32[]{:T(128)}, ...), condition=%wide.region_35.36_spmd, body=%wide.region_33.35_spmd.sunk | while | flops 869015040 | bytes 49660196 | solution.py:217
  1808.9 34.2 %all-gather.25.cloned.1.call-done = bf16[4,577,1024]{2,1,0:T(8,128)(2,1)} async-done(((bf16[1,577,1024]{2,1,0:T(8,128)(2,1)}), bf16[4,577,1024]{2,1,0:T(8,128)(2,1)}) %all-gather.25.cloned.1.call-update) | async-done | bytes 4726800 | tf_op jit(solution)/shard_map/all_gather | solution.py:210
  1858.7 53.2 %while.54 = (s32[]{:T(128)}, bf16[4,577,4,64]{1,3,2,0:T(8,128)(2,1)S(1)}, bf16[4,577,4,64]{1,3,2,0:T(8,128)(2,1)}, bf16[4,577,4,64]{1,3,2,0:T(8,128)(2,1)}, bf16...) while((s32[]{:T(128)}, ...), condition=%wide.region_26.27_spmd, body=%wide.region_24.26_spmd.sunk | while | flops 869015040 | bytes 49660196 | solution.py:217
  1952.0 9.5 fusion.183
  2025.6 79.9 %all-reduce.3.cloned.1.call-done = (f32[4,512,256]{1,2,0:T(8,128)}, f32[2,512,1024]{2,1,0:T(8,128)}) async-done(((f32[4,512,256]{1,2,0:T(8,128)}, f32[2,512,1024]{2,1,0:T(8,128)}), (f32[4,512,256]{1,2,0:T(8,128)}, f32[2,512,1024]{2,1,0:T(8,128)})) %all-reduce.3.cloned.1.call-update) | async-done | bytes 6291472 | tf_op jit(solution)/shard_map/psum | solution.py:282
  2120.4 13.2 fusion.262
  2133.6 12.4 pad_maximum_fusion
  2146.0 125.0 %reduce-scatter.21.cloned.1.call-done = f32[1,577,1024]{2,1,0:T(8,128)} async-done(((f32[4,577,1024]{2,1,0:T(8,128)}), f32[1,577,1024]{2,1,0:T(8,128)}) %reduce-scatter.21.cloned.1.call-update) | async-done | bytes 2363408 | tf_op jit(solution)/shard_map/reduce_scatter | solution.py:234
  2273.4 164.4 %reduce-scatter.25.cloned.1.call-done = f32[1,577,1024]{2,1,0:T(8,128)} async-done(((f32[4,577,1024]{2,1,0:T(8,128)}), f32[1,577,1024]{2,1,0:T(8,128)}) %reduce-scatter.25.cloned.1.call-update) | async-done | bytes 2363408 | tf_op jit(solution)/shard_map/reduce_scatter | solution.py:234
  2448.6 29.2 %psum.30 = f32[12,1024]{1,0:T(8,128)S(1)} all-reduce(f32[12,1024]{1,0:T(8,128)S(1)} %concatenate.7), channel_id=1, replica_groups=mesh['group'=4,'fsdp'=2,'tensor'=4] {'fsdp','tensor'}, use_global_device_ids=true, to_apply=%region_61.62 | all-reduce | flops 12288 | bytes 98304 | tf_op jit(solution)/shard_map/psum | solution.py:272
  2477.9 17.6 psum.31
  (482 shorter events, 518.1 us)
Async XLA Ops:
  7.2 16.3 all-gather.13.cloned.1.call-start
  10.1 107.3 %all-gather.19.cloned.1.call-start = ((), (), s32[]{:S(2)}) async-start(), calls=%async_computation.16 | async-start | bytes 5980160 | tf_op jit(solution)/shard_map/all_gather | solution.py:154
  19.3 189.2 %all-gather.11.cloned.1.call-start = ((), (), s32[]{:S(2)}) async-start(), calls=%async_computation.10 | async-start | bytes 5980160 | tf_op jit(solution)/shard_map/all_gather | solution.py:154
  20.0 415.1 %reduce-scatter.15.cloned.1.call-start = ((), (), s32[]{:S(2)}) async-start(), calls=%async_computation.17 | async-start | bytes 11960320 | tf_op jit(solution)/shard_map/reduce_scatter | solution.py:165
  273.1 329.1 %reduce-scatter.11.cloned.1.call-start = ((), (), s32[]{:S(2)}) async-start(), calls=%async_computation.12 | async-start | bytes 11960320 | tf_op jit(solution)/shard_map/reduce_scatter | solution.py:165
  308.4 293.9 %copy-start.65 = (f32[1,1024]{1,0:T(1,128)S(1)}, f32[1,1024]{1,0:T(1,128)}, u32[]{:S(2)}) copy-start(f32[1,1024]{1,0:T(1,128)} %get-tuple-element.393) | copy-start | bytes 12292
  308.4 320.9 %all-gather.17.cloned.1.call-start = ((), (), s32[]{:S(2)}) async-start(), calls=%async_computation.14 | async-start | bytes 6291456 | tf_op jit(solution)/shard_map/all_gather | solution.py:124
  312.3 400.3 %all-gather.21.cloned.1.call-start = ((), (), s32[]{:S(2)}) async-start(), calls=%async_computation.18 | async-start | bytes 5980160 | tf_op jit(solution)/shard_map/all_gather | solution.py:173
  609.2 194.6 %all-gather.15.cloned.1.call-start = ((), (), s32[]{:S(2)}) async-start(), calls=%async_computation.13 | async-start | bytes 5980160 | tf_op jit(solution)/shard_map/all_gather | solution.py:173
  609.9 284.4 %all-gather.23.cloned.1.call-start = ((), (), s32[]{:S(2)}) async-start(), calls=%async_computation.20 | async-start | bytes 5980160 | tf_op jit(solution)/shard_map/all_gather | solution.py:187
  623.7 361.1 %all-gather.27.cloned.1.call-start = ((), (), s32[]{:S(2)}) async-start(), calls=%async_computation.24 | async-start | bytes 5980160 | tf_op jit(solution)/shard_map/all_gather | solution.py:187
  628.2 520.7 %reduce-scatter.19.cloned.1.call-start = ((), (), s32[]{:S(2)}) async-start(), calls=%async_computation.21 | async-start | bytes 11960320 | tf_op jit(solution)/shard_map/reduce_scatter | solution.py:199
  916.9 398.6 %reduce-scatter.23.cloned.1.call-start = ((), (), s32[]{:S(2)}) async-start(), calls=%async_computation.25 | async-start | bytes 11960320 | tf_op jit(solution)/shard_map/reduce_scatter | solution.py:199
  1007.0 475.1 %reduce-scatter.13.cloned.1.call-start = ((), (), s32[]{:S(2)}) async-start(), calls=%async_computation.15 | async-start | bytes 11960320 | tf_op jit(solution)/shard_map/reduce_scatter | solution.py:179
  1063.8 585.5 %reduce-scatter.17.cloned.1.call-start = ((), (), s32[]{:S(2)}) async-start(), calls=%async_computation.19 | async-start | bytes 11960320 | tf_op jit(solution)/shard_map/reduce_scatter | solution.py:179
  1074.4 574.9 %copy-start.63 = (f32[1,1024]{1,0:T(1,128)S(1)}, f32[1,1024]{1,0:T(1,128)}, u32[]{:S(2)}) copy-start(f32[1,1024]{1,0:T(1,128)} %get-tuple-element.390) | copy-start | bytes 12292
  1074.4 677.7 %all-gather.29.cloned.1.call-start = ((), (), s32[]{:S(2)}) async-start(), calls=%async_computation.26 | async-start | bytes 5980160 | tf_op jit(solution)/shard_map/all_gather | solution.py:210
  1660.6 182.5 %all-gather.25.cloned.1.call-start = ((), (), s32[]{:S(2)}) async-start(), calls=%async_computation.22 | async-start | bytes 5980160 | tf_op jit(solution)/shard_map/all_gather | solution.py:210
  1665.2 286.8 %reduce-scatter.29.cloned.1.call-start = ((), (), s32[]{:S(2)}) async-start(), calls=%async_computation.29 | async-start | bytes 12582912 | tf_op jit(solution)/shard_map/reduce_scatter | solution.py:264
  1700.6 261.0 %reduce-scatter.27.cloned.1.call-start = ((), (), s32[]{:S(2)}) async-start(), calls=%async_computation.28 | async-start | bytes 6291456 | tf_op jit(solution)/shard_map/reduce_scatter | solution.py:263
  1937.4 168.1 %all-reduce.3.cloned.1.call-start = ((), (), s32[]{:S(2)}) async-start(), calls=%async_computation.30 | async-start | bytes 12582912 | tf_op jit(solution)/shard_map/psum | solution.py:282
  1968.6 302.4 %reduce-scatter.21.cloned.1.call-start = ((), (), s32[]{:S(2)}) async-start(), calls=%async_computation.23 | async-start | bytes 11960320 | tf_op jit(solution)/shard_map/reduce_scatter | solution.py:234
  1981.9 456.0 %reduce-scatter.25.cloned.1.call-start = ((), (), s32[]{:S(2)}) async-start(), calls=%async_computation.27 | async-start | bytes 11960320 | tf_op jit(solution)/shard_map/reduce_scatter | solution.py:234
  2133.6 137.4 %copy-start.4 = (bf16[1,1,1,577,1024]{4,3,2,1,0:T(8,128)(2,1)S(1)}, bf16[1,1,1,577,1024]{4,3,2,1,0:T(8,128)(2,1)}, u32[]{:S(2)}) copy-start(bf16[1,1,1,577,1024]{4,3,2,1,0:T(8,128)(2,1)} %copy-done.3) | copy-start | bytes 3545092
  2133.6 137.4 %copy-start.41 = (f32[1,1024]{1,0:T(1,128)S(1)}, f32[1,1024]{1,0:T(1,128)}, u32[]{:S(2)}) copy-start(f32[1,1024]{1,0:T(1,128)} %copy-done.40) | copy-start | bytes 12292
  2133.6 137.4 %copy-start.43 = (f32[577]{0:T(1024)S(1)}, f32[577]{0:T(1024)}, u32[]{:S(2)}) copy-start(f32[577]{0:T(1024)} %copy-done.42) | copy-start | bytes 6928
  2146.0 291.8 %copy-start.2 = (bf16[1,1,1,577,1024]{4,3,2,1,0:T(8,128)(2,1)S(1)}, bf16[1,1,1,577,1024]{4,3,2,1,0:T(8,128)(2,1)}, u32[]{:S(2)}) copy-start(bf16[1,1,1,577,1024]{4,3,2,1,0:T(8,128)(2,1)} %copy-done.1) | copy-start | bytes 3545092
  2146.0 291.8 %copy-start.39 = (f32[577]{0:T(1024)S(1)}, f32[577]{0:T(1024)}, u32[]{:S(2)}) copy-start(f32[577]{0:T(1024)} %copy-done.38) | copy-start | bytes 6928
  2146.0 291.8 %copy-start.49 = (f32[577]{0:T(1024)S(1)}, f32[577]{0:T(1024)}, u32[]{:S(2)}) copy-start(f32[577]{0:T(1024)} %copy-done.48) | copy-start | bytes 6928
  2273.4 168.6 %copy-start.52 = (f32[577]{0:T(1024)S(1)}, f32[577]{0:T(1024)}, u32[]{:S(2)}) copy-start(f32[577]{0:T(1024)} %copy-done.51) | copy-start | bytes 6928
  2273.4 168.7 %copy-start.47 = (f32[577]{0:T(1024)S(1)}, f32[577]{0:T(1024)}, u32[]{:S(2)}) copy-start(f32[577]{0:T(1024)} %copy-done.46) | copy-start | bytes 6928
  2273.4 168.7 %copy-start.58 = (f32[577]{0:T(1024)S(1)}, f32[577]{0:T(1024)}, u32[]{:S(2)}) copy-start(f32[577]{0:T(1024)} %copy-done.57) | copy-start | bytes 6928
  (86 other events, 780.0 us)
Sparse Core Ops, SparseCore 0:
  10.2 13.2 all-gather.12
  25.6 91.6 all-gather.18
  119.5 88.9 all-gather.10
  273.3 161.7 reduce-scatter.14
  438.0 164.2 reduce-scatter.10
  604.3 14.5 all-gather.16
  620.9 91.6 all-gather.20
  714.8 88.9 all-gather.14
  805.4 88.9 all-gather.22
  895.7 88.9 all-gather.26
  987.1 161.7 reduce-scatter.18
  1151.2 164.2 reduce-scatter.22
  1317.9 164.2 reduce-scatter.12
  1485.0 164.2 reduce-scatter.16
  1660.7 91.3 all-gather.28
  1754.1 88.9 all-gather.24
  1845.8 15.2 reduce-scatter.28
  1937.5 10.6 reduce-scatter.26
  1968.8 136.6 all-reduce.2
  2107.6 163.3 reduce-scatter.20
  2273.5 164.2 reduce-scatter.24
where the time goes:
time: 2530 us; the launch traced here: 2520 us
  waiting for transfers between devices  1800 us (71%)
  matrix products  322 us (13%)
  other arithmetic  213 us (8%)
  local copies, waits for them, and re-layouts  124 us (5%)
  blocking collectives  46.8 us (2%)
    reduce_scatter x2, waiting for transfers between devices, local(): lax.psum_scatter(jnp.einsum('isf,df->isd', hidden, mlp_all[1], preferred_...  329 us
    reduce_scatter x2, waiting for transfers between devices, local(): lax.psum_scatter(jnp.einsum('ise,de->isd', attended, attn_all[3], preferr...  290 us
    reduce_scatter x2, waiting for transfers between devices, local(): lax.psum_scatter(summed + jnp.einsum('ise,de->isd', grad_values, attn_all...  289 us
    reduce_scatter x2, waiting for transfers between devices, local(): lax.psum_scatter(jnp.einsum('isf,df->isd', grad_pre, mlp_all[0], preferre...  241 us
    all_gather x2, waiting for transfers between devices, local(): rows_attn = lax.all_gather(normed_one, 'tensor', axis=0, tiled=True)  176 us
    all_gather x2, waiting for transfers between devices, local(): rows_mlp = lax.all_gather(normed_two, 'tensor', axis=0, tiled=True)  164 us
    all_gather x2, waiting for transfers between devices, local(): lax.all_gather(grad_out.astype(narrow), 'tensor', axis=0, tiled=True)  138 us
    all_gather x2, waiting for transfers between devices, local(): lax.all_gather(grad_resid.astype(narrow), 'tensor', axis=0, tiled=True)  85.5 us
  transfers between devices with their start and end apart: 21, of which 18 were waited for; matrix products, arithmetic and copies ran while one was open for 21% of the time, Pallas kernels for 0%

commit v1 on v0

--- a/solution.py
+++ b/solution.py
@@ -151,7 +151,16 @@
         inputs = patches[0, batch_index].astype(single)
         alive = alive_all[batch_index][:, None, None]
         normed_one = normalize(inputs, vector_master[0], vector_master[1]).astype(narrow)
-        rows_attn = lax.all_gather(normed_one, "tensor", axis=0, tiled=True)
+        ring = [normed_one]
+        for hop in range(3):
+            ring.append(
+                lax.ppermute(ring[-1], "tensor", [(dev, (dev + 1) % 4) for dev in range(4)])
+            )
+        rows_attn = jnp.roll(
+            jnp.concatenate(ring[::-1], axis=0),
+            (lax.axis_index("tensor") + 1) * ring[0].shape[0],
+            axis=0,
+        )
         image_count = rows_attn.shape[0]
         shape_heads = (image_count, seq_len, heads_here, HD)
         projected = jnp.einsum(

time: 2530 us -> 2500 us (0.988)
  waiting for transfers between devices: 1800 us -> 1750 us
    all_gather x2 -> x0, waiting for transfers between devices: 176 us -> none  [local(): rows_attn = lax.all_gather(normed_one, 'tensor', axis=0, tiled=True)]
    ppermute x0 -> x6, waiting for transfers between devices: none -> 129 us  [local(): lax.ppermute(ring[-1], 'tensor', [(dev, (dev + 1) % 4) for dev in range(4)])]
    unnamed x189 -> x199, local copies, waits for them, and re-layouts: 50.9 us -> 50.3 us
  transfers between devices with their start and end apart: 21 -> 25, of which waited for: 18 -> 21; matrix products, arithmetic and copies ran while one was open for 21% -> 22% of each run, Pallas kernels for 0% -> 0%
where the time goes in v1:
time: 2500 us
  waiting for transfers between devices  1750 us (70%)
  matrix products  320 us (13%)
  other arithmetic  232 us (9%)
  local copies, waits for them, and re-layouts  122 us (5%)
  blocking collectives  46.9 us (2%)
    reduce_scatter x2, waiting for transfers between devices, local(): lax.psum_scatter(jnp.einsum('isf,df->isd', hidden, mlp_all[1], preferred_...  329 us
    reduce_scatter x2, waiting for transfers between devices, local(): lax.psum_scatter(jnp.einsum('ise,de->isd', attended, attn_all[3], preferr...  294 us
    reduce_scatter x2, waiting for transfers between devices, local(): lax.psum_scatter(summed + jnp.einsum('ise,de->isd', grad_values, attn_all...  290 us
    reduce_scatter x2, waiting for transfers between devices, local(): lax.psum_scatter(jnp.einsum('isf,df->isd', grad_pre, mlp_all[0], preferre...  241 us
    all_gather x2, waiting for transfers between devices, local(): rows_mlp = lax.all_gather(normed_two, 'tensor', axis=0, tiled=True)  164 us
    all_gather x2, waiting for transfers between devices, local(): lax.all_gather(grad_out.astype(narrow), 'tensor', axis=0, tiled=True)  138 us
    ppermute x6, waiting for transfers between devices, local(): lax.ppermute(ring[-1], 'tensor', [(dev, (dev + 1) % 4) for dev in range(4)])  129 us
    all_gather x2, waiting for transfers between devices, local(): lax.all_gather(grad_resid.astype(narrow), 'tensor', axis=0, tiled=True)  85.7 us
  transfers between devices with their start and end apart: 25, of which 21 were waited for; matrix products, arithmetic and copies ran while one was open for 22% of the time, Pallas kernels for 0%

profile of v1, /device:TPU:0, one launch (start us, length us, event | category | flops | bytes accessed | tf_op | source)
XLA Modules:
  0.0 2495.5 jit_solution(10322715845299574453)
XLA Ops:
  22.4 27.6 %collective-permute-done.3 = bf16[1,577,1024]{2,1,0:T(8,128)(2,1)S(1)} collective-permute-done((bf16[1,577,1024]{2,1,0:T(8,128)(2,1)S(1)}, bf16[1,577,1024]{2,1,0:T(8,128)(2,1)S(1)}, u32[]{:S(2)}, u32[]{:S(2)}) %collective-permute-start.3) | collective-permute-done | bytes 1181728 | tf_op jit(solution)/shard_map/ppermute | solution.py:157
  50.0 25.6 %collective-permute-done = bf16[1,577,1024]{2,1,0:T(8,128)(2,1)S(1)} collective-permute-done((bf16[1,577,1024]{2,1,0:T(8,128)(2,1)S(1)}, bf16[1,577,1024]{2,1,0:T(8,128)(2,1)S(1)}, u32[]{:S(2)}, u32[]{:S(2)}) %collective-permute-start) | collective-permute-done | bytes 1181728 | tf_op jit(solution)/shard_map/ppermute | solution.py:157
  75.6 25.7 %collective-permute-done.4 = bf16[1,577,1024]{2,1,0:T(8,128)(2,1)} collective-permute-done((bf16[1,577,1024]{2,1,0:T(8,128)(2,1)S(1)}, bf16[1,577,1024]{2,1,0:T(8,128)(2,1)}, u32[]{:S(2)}, u32[]{:S(2)}) %collective-permute-start.4) | collective-permute-done | bytes 1181728 | tf_op jit(solution)/shard_map/ppermute | solution.py:157
  102.7 24.2 collective-permute-done.1
  127.2 25.4 %collective-permute-done.5 = bf16[1,577,1024]{2,1,0:T(8,128)(2,1)} collective-permute-done((bf16[1,577,1024]{2,1,0:T(8,128)(2,1)}, bf16[1,577,1024]{2,1,0:T(8,128)(2,1)}, u32[]{:S(2)}, u32[]{:S(2)}) %collective-permute-start.5) | collective-permute-done | bytes 1181728 | tf_op jit(solution)/shard_map/ppermute | solution.py:157
  214.2 21.4 while.53
  246.4 22.6 while.52
  280.0 126.4 %reduce-scatter.15.cloned.1.call-done = f32[1,577,1024]{2,1,0:T(8,128)} async-done(((f32[4,577,1024]{2,1,0:T(8,128)}), f32[1,577,1024]{2,1,0:T(8,128)}) %reduce-scatter.15.cloned.1.call-update) | async-done | bytes 2363408 | tf_op jit(solution)/shard_map/reduce_scatter | solution.py:174
  406.4 167.3 %reduce-scatter.11.cloned.1.call-done = f32[1,577,1024]{2,1,0:T(8,128)} async-done(((f32[4,577,1024]{2,1,0:T(8,128)}), f32[1,577,1024]{2,1,0:T(8,128)}) %reduce-scatter.11.cloned.1.call-update) | async-done | bytes 2363408 | tf_op jit(solution)/shard_map/reduce_scatter | solution.py:174
  600.4 83.6 %all-gather.15.cloned.1.call-done = bf16[4,577,1024]{2,1,0:T(8,128)(2,1)} async-done(((bf16[1,577,1024]{2,1,0:T(8,128)(2,1)}), bf16[4,577,1024]{2,1,0:T(8,128)(2,1)}) %all-gather.15.cloned.1.call-update) | async-done | bytes 4726800 | tf_op jit(solution)/shard_map/all_gather | solution.py:182
  694.3 80.7 %all-gather.11.cloned.1.call-done = bf16[4,577,1024]{2,1,0:T(8,128)(2,1)} async-done(((bf16[1,577,1024]{2,1,0:T(8,128)(2,1)}), bf16[4,577,1024]{2,1,0:T(8,128)(2,1)}) %all-gather.11.cloned.1.call-update) | async-done | bytes 4726800 | tf_op jit(solution)/shard_map/all_gather | solution.py:182
  775.0 20.2 fusion.224
  795.2 70.4 %all-gather.17.cloned.1.call-done = bf16[4,577,1024]{2,1,0:T(8,128)(2,1)} async-done(((bf16[1,577,1024]{2,1,0:T(8,128)(2,1)}), bf16[4,577,1024]{2,1,0:T(8,128)(2,1)}) %all-gather.17.cloned.1.call-update) | async-done | bytes 4726800 | tf_op jit(solution)/shard_map/all_gather | solution.py:196
  865.5 12.3 convert_reduce_fusion.1
  888.2 67.8 %all-gather.21.cloned.1.call-done = bf16[4,577,1024]{2,1,0:T(8,128)(2,1)} async-done(((bf16[1,577,1024]{2,1,0:T(8,128)(2,1)}), bf16[4,577,1024]{2,1,0:T(8,128)(2,1)}) %all-gather.21.cloned.1.call-update) | async-done | bytes 4726800 | tf_op jit(solution)/shard_map/all_gather | solution.py:196
  956.1 12.6 convert_reduce_fusion
  978.5 46.6 %fusion.116 = (bf16[4,577,1024]{2,1,0:T(8,128)(2,1)S(1)}, bf16[4,577,1024]{2,1,0:T(8,128)(2,1)}) fusion(f32[4,577,1024]{2,1,0:T(8,128)} %get-tuple-element.422, f32[1024]{0:T(1024)S(1)} %dynamic_slice.64, u8[577,1024]{1,0:T(8,128)(4,1)} %get-tuple-element.250, u8[577,1024]{1,0:T(8,128)(4,1)S(1)} %get-tuple-element.249, ...), kind=kLoop, calls=%fused_computation.127 | loop fusion | flops 333238272 | bytes 30728192 | tf_op jit(solution)/shard_map/convert_element_type | solution.py:187
  1045.8 74.5 %reduce-scatter.19.cloned.1.call-done = f32[1,577,1024]{2,1,0:T(8,128)} async-done(((f32[4,577,1024]{2,1,0:T(8,128)}), f32[1,577,1024]{2,1,0:T(8,128)}) %reduce-scatter.19.cloned.1.call-update) | async-done | bytes 2363408 | tf_op jit(solution)/shard_map/reduce_scatter | solution.py:208
  1120.3 166.6 %reduce-scatter.23.cloned.1.call-done = f32[1,577,1024]{2,1,0:T(8,128)} async-done(((f32[4,577,1024]{2,1,0:T(8,128)}), f32[1,577,1024]{2,1,0:T(8,128)}) %reduce-scatter.23.cloned.1.call-update) | async-done | bytes 2363408 | tf_op jit(solution)/shard_map/reduce_scatter | solution.py:208
  1292.2 161.3 %reduce-scatter.13.cloned.1.call-done = f32[1,577,1024]{2,1,0:T(8,128)} async-done(((f32[4,577,1024]{2,1,0:T(8,128)}), f32[1,577,1024]{2,1,0:T(8,128)}) %reduce-scatter.13.cloned.1.call-update) | async-done | bytes 2363408 | tf_op jit(solution)/shard_map/reduce_scatter | solution.py:188
  1453.5 167.2 %reduce-scatter.17.cloned.1.call-done = f32[1,577,1024]{2,1,0:T(8,128)} async-done(((f32[4,577,1024]{2,1,0:T(8,128)}), f32[1,577,1024]{2,1,0:T(8,128)}) %reduce-scatter.17.cloned.1.call-update) | async-done | bytes 2363408 | tf_op jit(solution)/shard_map/reduce_scatter | solution.py:188
  1672.1 51.5 %all-gather.19.cloned.1.call-done = bf16[4,577,1024]{2,1,0:T(8,128)(2,1)} async-done(((bf16[1,577,1024]{2,1,0:T(8,128)(2,1)}), bf16[4,577,1024]{2,1,0:T(8,128)(2,1)}) %all-gather.19.cloned.1.call-update) | async-done | bytes 4726800 | tf_op jit(solution)/shard_map/all_gather | solution.py:219
  1731.6 48.7 %while.54 = (s32[]{:T(128)}, bf16[4,577,4,64]{1,3,2,0:T(8,128)(2,1)S(1)}, bf16[4,577,4,64]{1,3,2,0:T(8,128)(2,1)}, bf16[4,577,4,64]{1,3,2,0:T(8,128)(2,1)}, bf16...) while((s32[]{:T(128)}, ...), condition=%wide.region_26.28_spmd, body=%wide.region_24.27_spmd.sunk | while | flops 869015040 | bytes 49660196 | solution.py:226
  1780.3 34.2 %all-gather.23.cloned.1.call-done = bf16[4,577,1024]{2,1,0:T(8,128)(2,1)} async-done(((bf16[1,577,1024]{2,1,0:T(8,128)(2,1)}), bf16[4,577,1024]{2,1,0:T(8,128)(2,1)}) %all-gather.23.cloned.1.call-update) | async-done | bytes 4726800 | tf_op jit(solution)/shard_map/all_gather | solution.py:219
  1830.2 53.2 %while.55 = (s32[]{:T(128)}, bf16[4,577,4,64]{1,3,2,0:T(8,128)(2,1)S(1)}, bf16[4,577,4,64]{1,3,2,0:T(8,128)(2,1)}, bf16[4,577,4,64]{1,3,2,0:T(8,128)(2,1)}, bf16...) while((s32[]{:T(128)}, ...), condition=%wide.region_35.37_spmd, body=%wide.region_33.36_spmd.sunk | while | flops 869015040 | bytes 49660196 | solution.py:226
  1999.9 79.8 %all-reduce.3.cloned.1.call-done = (f32[4,512,256]{1,2,0:T(8,128)}, f32[2,512,1024]{2,1,0:T(8,128)}) async-done(((f32[4,512,256]{1,2,0:T(8,128)}, f32[2,512,1024]{2,1,0:T(8,128)}), (f32[4,512,256]{1,2,0:T(8,128)}, f32[2,512,1024]{2,1,0:T(8,128)})) %all-reduce.3.cloned.1.call-update) | async-done | bytes 6291472 | tf_op jit(solution)/shard_map/psum | solution.py:291
  2094.5 13.2 fusion.278
  2107.7 12.4 pad_maximum_fusion
  2120.1 125.2 %reduce-scatter.21.cloned.1.call-done = f32[1,577,1024]{2,1,0:T(8,128)} async-done(((f32[4,577,1024]{2,1,0:T(8,128)}), f32[1,577,1024]{2,1,0:T(8,128)}) %reduce-scatter.21.cloned.1.call-update) | async-done | bytes 2363408 | tf_op jit(solution)/shard_map/reduce_scatter | solution.py:243
  2247.6 164.4 %reduce-scatter.25.cloned.1.call-done = f32[1,577,1024]{2,1,0:T(8,128)} async-done(((f32[4,577,1024]{2,1,0:T(8,128)}), f32[1,577,1024]{2,1,0:T(8,128)}) %reduce-scatter.25.cloned.1.call-update) | async-done | bytes 2363408 | tf_op jit(solution)/shard_map/reduce_scatter | solution.py:243
  2422.9 29.2 %psum.30 = f32[12,1024]{1,0:T(8,128)S(1)} all-reduce(f32[12,1024]{1,0:T(8,128)S(1)} %concatenate.18), channel_id=1, replica_groups=mesh['group'=4,'fsdp'=2,'tensor'=4] {'fsdp','tensor'}, use_global_device_ids=true, to_apply=%region_61.63 | all-reduce | flops 12288 | bytes 98304 | tf_op jit(solution)/shard_map/psum | solution.py:281
  2452.2 17.7 psum.31
  (499 shorter events, 565.2 us)
Async XLA Ops:
  7.2 156.8 %all-gather.9.cloned.1.call-start = ((), (), s32[]{:S(2)}) async-start(), calls=%async_computation.10 | async-start | bytes 3145728 | tf_op jit(solution)/shard_map/all_gather | solution.py:123
  17.7 32.2 %collective-permute-start.3 = (bf16[1,577,1024]{2,1,0:T(8,128)(2,1)S(1)}, bf16[1,577,1024]{2,1,0:T(8,128)(2,1)S(1)}, u32[]{:S(2)}, u32[]{:S(2)}) collective-permute-start(bf16[1,577,1024]{2,1,0:T(8,128)(2,1)S(1)} %get-tuple-element.405), channel_id=1, source_target_pairs={{0,1},{1,2},{2,3},{3,0},{4,5},{5,6},{6,7},{7,4},{8,9},{9,10},{10,1... | collective-permute-start | bytes 3545096 | tf_op jit(solution)/shard_map/ppermute | solution.py:157
  20.8 54.8 %collective-permute-start = (bf16[1,577,1024]{2,1,0:T(8,128)(2,1)S(1)}, bf16[1,577,1024]{2,1,0:T(8,128)(2,1)S(1)}, u32[]{:S(2)}, u32[]{:S(2)}) collective-permute-start(bf16[1,577,1024]{2,1,0:T(8,128)(2,1)S(1)} %get-tuple-element.404), channel_id=1, source_target_pairs={{0,1},{1,2},{2,3},{3,0},{4,5},{5,6},{6,7},{7,4},{8,9},{9,10},{10,1... | collective-permute-start | bytes 3545096 | tf_op jit(solution)/shard_map/ppermute | solution.py:157
  49.9 51.4 %collective-permute-start.4 = (bf16[1,577,1024]{2,1,0:T(8,128)(2,1)S(1)}, bf16[1,577,1024]{2,1,0:T(8,128)(2,1)}, u32[]{:S(2)}, u32[]{:S(2)}) collective-permute-start(bf16[1,577,1024]{2,1,0:T(8,128)(2,1)S(1)} %collective-permute-done.3), channel_id=1, source_target_pairs={{0,1},{1,2},{2,3},{3,0},{4,5},{5,6},{6,7},{7,4},{8,9},{9,10},{10,1... | collective-permute-start | bytes 3545096 | tf_op jit(solution)/shard_map/ppermute | solution.py:157
  75.6 51.4 %collective-permute-start.1 = (bf16[1,577,1024]{2,1,0:T(8,128)(2,1)S(1)}, bf16[1,577,1024]{2,1,0:T(8,128)(2,1)}, u32[]{:S(2)}, u32[]{:S(2)}) collective-permute-start(bf16[1,577,1024]{2,1,0:T(8,128)(2,1)S(1)} %collective-permute-done), channel_id=1, source_target_pairs={{0,1},{1,2},{2,3},{3,0},{4,5},{5,6},{6,7},{7,4},{8,9},{9,10},{10,1... | collective-permute-start | bytes 3545096 | tf_op jit(solution)/shard_map/ppermute | solution.py:157
  101.3 51.3 %collective-permute-start.5 = (bf16[1,577,1024]{2,1,0:T(8,128)(2,1)}, bf16[1,577,1024]{2,1,0:T(8,128)(2,1)}, u32[]{:S(2)}, u32[]{:S(2)}) collective-permute-start(bf16[1,577,1024]{2,1,0:T(8,128)(2,1)} %collective-permute-done.4), channel_id=1, source_target_pairs={{0,1},{1,2},{2,3},{3,0},{4,5},{5,6},{6,7},{7,4},{8,9},{9,10},{10,1... | collective-permute-start | bytes 3545096 | tf_op jit(solution)/shard_map/ppermute | solution.py:157
  102.4 304.0 %reduce-scatter.15.cloned.1.call-start = ((), (), s32[]{:S(2)}) async-start(), calls=%async_computation.15 | async-start | bytes 11960320 | tf_op jit(solution)/shard_map/reduce_scatter | solution.py:174
  126.9 50.4 %collective-permute-start.2 = (bf16[1,577,1024]{2,1,0:T(8,128)(2,1)}, bf16[1,577,1024]{2,1,0:T(8,128)(2,1)}, u32[]{:S(2)}, u32[]{:S(2)}) collective-permute-start(bf16[1,577,1024]{2,1,0:T(8,128)(2,1)} %collective-permute-done.1), channel_id=1, source_target_pairs={{0,1},{1,2},{2,3},{3,0},{4,5},{5,6},{6,7},{7,4},{8,9},{9,10},{10,1... | collective-permute-start | bytes 3545096 | tf_op jit(solution)/shard_map/ppermute | solution.py:157
  243.5 330.3 %reduce-scatter.11.cloned.1.call-start = ((), (), s32[]{:S(2)}) async-start(), calls=%async_computation.11 | async-start | bytes 11960320 | tf_op jit(solution)/shard_map/reduce_scatter | solution.py:174
  276.0 297.7 %copy-start.73 = (f32[1,1024]{1,0:T(1,128)S(1)}, f32[1,1024]{1,0:T(1,128)}, u32[]{:S(2)}) copy-start(f32[1,1024]{1,0:T(1,128)} %get-tuple-element.394) | copy-start | bytes 12292
  276.0 324.4 %all-gather.13.cloned.1.call-start = ((), (), s32[]{:S(2)}) async-start(), calls=%async_computation.13 | async-start | bytes 6291456 | tf_op jit(solution)/shard_map/all_gather | solution.py:124
  279.9 404.1 %all-gather.15.cloned.1.call-start = ((), (), s32[]{:S(2)}) async-start(), calls=%async_computation.16 | async-start | bytes 5980160 | tf_op jit(solution)/shard_map/all_gather | solution.py:182
  580.6 194.4 %all-gather.11.cloned.1.call-start = ((), (), s32[]{:S(2)}) async-start(), calls=%async_computation.12 | async-start | bytes 5980160 | tf_op jit(solution)/shard_map/all_gather | solution.py:182
  581.2 284.3 %all-gather.17.cloned.1.call-start = ((), (), s32[]{:S(2)}) async-start(), calls=%async_computation.18 | async-start | bytes 5980160 | tf_op jit(solution)/shard_map/all_gather | solution.py:196
  594.9 361.2 %all-gather.21.cloned.1.call-start = ((), (), s32[]{:S(2)}) async-start(), calls=%async_computation.22 | async-start | bytes 5980160 | tf_op jit(solution)/shard_map/all_gather | solution.py:196
  599.4 520.9 %reduce-scatter.19.cloned.1.call-start = ((), (), s32[]{:S(2)}) async-start(), calls=%async_computation.19 | async-start | bytes 11960320 | tf_op jit(solution)/shard_map/reduce_scatter | solution.py:208
  888.2 398.7 %reduce-scatter.23.cloned.1.call-start = ((), (), s32[]{:S(2)}) async-start(), calls=%async_computation.23 | async-start | bytes 11960320 | tf_op jit(solution)/shard_map/reduce_scatter | solution.py:208
  978.4 475.1 %reduce-scatter.13.cloned.1.call-start = ((), (), s32[]{:S(2)}) async-start(), calls=%async_computation.14 | async-start | bytes 11960320 | tf_op jit(solution)/shard_map/reduce_scatter | solution.py:188
  1035.0 585.6 %reduce-scatter.17.cloned.1.call-start = ((), (), s32[]{:S(2)}) async-start(), calls=%async_computation.17 | async-start | bytes 11960320 | tf_op jit(solution)/shard_map/reduce_scatter | solution.py:188
  1045.7 575.0 %copy-start.71 = (f32[1,1024]{1,0:T(1,128)S(1)}, f32[1,1024]{1,0:T(1,128)}, u32[]{:S(2)}) copy-start(f32[1,1024]{1,0:T(1,128)} %get-tuple-element.391) | copy-start | bytes 12292
  1045.7 677.9 %all-gather.19.cloned.1.call-start = ((), (), s32[]{:S(2)}) async-start(), calls=%async_computation.20 | async-start | bytes 5980160 | tf_op jit(solution)/shard_map/all_gather | solution.py:219
  1632.1 182.5 %all-gather.23.cloned.1.call-start = ((), (), s32[]{:S(2)}) async-start(), calls=%async_computation.24 | async-start | bytes 5980160 | tf_op jit(solution)/shard_map/all_gather | solution.py:219
  1636.6 289.5 %reduce-scatter.29.cloned.1.call-start = ((), (), s32[]{:S(2)}) async-start(), calls=%async_computation.27 | async-start | bytes 12582912 | tf_op jit(solution)/shard_map/reduce_scatter | solution.py:273
  1671.9 263.7 %reduce-scatter.27.cloned.1.call-start = ((), (), s32[]{:S(2)}) async-start(), calls=%async_computation.26 | async-start | bytes 6291456 | tf_op jit(solution)/shard_map/reduce_scatter | solution.py:272
  1911.8 167.9 %all-reduce.3.cloned.1.call-start = ((), (), s32[]{:S(2)}) async-start(), calls=%async_computation.28 | async-start | bytes 12582912 | tf_op jit(solution)/shard_map/psum | solution.py:291
  1942.7 302.6 %reduce-scatter.21.cloned.1.call-start = ((), (), s32[]{:S(2)}) async-start(), calls=%async_computation.21 | async-start | bytes 11960320 | tf_op jit(solution)/shard_map/reduce_scatter | solution.py:243
  1956.2 455.9 %reduce-scatter.25.cloned.1.call-start = ((), (), s32[]{:S(2)}) async-start(), calls=%async_computation.25 | async-start | bytes 11960320 | tf_op jit(solution)/shard_map/reduce_scatter | solution.py:243
  2120.1 292.0 %copy-start.2 = (bf16[1,1,1,577,1024]{4,3,2,1,0:T(8,128)(2,1)S(1)}, bf16[1,1,1,577,1024]{4,3,2,1,0:T(8,128)(2,1)}, u32[]{:S(2)}) copy-start(bf16[1,1,1,577,1024]{4,3,2,1,0:T(8,128)(2,1)} %copy-done.1) | copy-start | bytes 3545092
  2120.1 292.0 %copy-start.47 = (f32[577]{0:T(1024)S(1)}, f32[577]{0:T(1024)}, u32[]{:S(2)}) copy-start(f32[577]{0:T(1024)} %copy-done.46) | copy-start | bytes 6928
  2120.1 292.0 %copy-start.57 = (f32[577]{0:T(1024)S(1)}, f32[577]{0:T(1024)}, u32[]{:S(2)}) copy-start(f32[577]{0:T(1024)} %copy-done.56) | copy-start | bytes 6928
  2247.6 168.7 %copy-start.55 = (f32[577]{0:T(1024)S(1)}, f32[577]{0:T(1024)}, u32[]{:S(2)}) copy-start(f32[577]{0:T(1024)} %copy-done.54) | copy-start | bytes 6928
  2247.6 168.7 %copy-start.66 = (f32[577]{0:T(1024)S(1)}, f32[577]{0:T(1024)}, u32[]{:S(2)}) copy-start(f32[577]{0:T(1024)} %copy-done.65) | copy-start | bytes 6928
  (95 other events, 1580.9 us)
Sparse Core Ops, SparseCore 0:
  102.6 12.2 all-gather.8
  243.6 162.7 reduce-scatter.14
  409.5 164.2 reduce-scatter.10
  575.7 14.5 all-gather.12
  592.3 91.6 all-gather.14
  686.0 88.9 all-gather.10
  776.6 88.9 all-gather.16
  867.1 88.9 all-gather.20
  958.4 161.7 reduce-scatter.18
  1122.6 164.2 reduce-scatter.22
  1289.3 164.1 reduce-scatter.12
  1456.4 164.2 reduce-scatter.16
  1632.2 91.3 all-gather.18
  1725.6 88.9 all-gather.22
  1817.3 15.2 reduce-scatter.28
  1911.9 10.6 reduce-scatter.26
  1942.9 136.7 all-reduce.2
  2081.9 163.3 reduce-scatter.20
  2247.8 164.2 reduce-scatter.24
